TPU v7x, 128 devices: a whole 4x4x4 slice. The times are simulated.
128 devices in a mesh: farcp: 4 (over x_lo, core), nearcp: 4 (over z_lo, x_hi), heads: 8 (over z_hi, y).
Axes of the slice: x: 4 (x_hi: 2, x_lo: 2; x = x_hi * 2 + x_lo), y: 4, z: 4 (z_hi: 2, z_lo: 2; z = z_hi * 2 + z_lo), core: 2. Of those that a mesh axis runs over, the one named last changes fastest.
Arguments:
- raw_keys: bfloat16 [16, 24576, 8, 128], P(None, ('farcp', 'nearcp'), 'heads'), may hold values from -6 to 6
- raw_values: bfloat16 [16, 24576, 8, 128], P(None, ('farcp', 'nearcp'), 'heads'), may hold values from -6 to 6
- turn_angle: float32 [24576, 64], replicated, may hold values from -3.140625 to 3.140625
Outputs:
- stored_keys: bfloat16 [16, 8, 128, 24576], P(('farcp', 'nearcp'), 'heads')
- stored_values: bfloat16 [16, 24576, 8, 128], P(('farcp', 'nearcp'), None, 'heads')
- page_high: bfloat16 [16, 384, 8, 128], P(('farcp', 'nearcp'), None, 'heads')
- page_low: bfloat16 [16, 384, 8, 128], P(('farcp', 'nearcp'), None, 'heads')
All inputs are finite; a program needn't handle non-finite values.
Results may differ from a plain program's by a relative error of at most 0.001.
Values may be sent and summed in bfloat16 or wider, within the bound.
A program may use at most 128 MiB of HBM per device.

v0:
```python
import jax
import jax.numpy as jnp
from jax import lax
from jax.sharding import PartitionSpec as P

PAGE = 64


def in_one_piece(arrays, axis, split_dim, concat_dim, along):
    both = jnp.concatenate(arrays, axis=along)
    filled, at, finished = (
        lax.all_to_all(both, axis, split_axis=split_dim, concat_axis=concat_dim, tiled=True),
        0,
        [],
    )
    for a in arrays:
        finished.append(lax.slice_in_dim(filled, at, at + a.shape[along], axis=along))
        at += a.shape[along]
    return tuple(finished)


def apply_rotary(vectors, angle):
    half = vectors.shape[-1] // 2
    cosine, sine = (jnp.cos(angle)[None, :, None, :], jnp.sin(angle)[None, :, None, :])
    first, second = (vectors[..., :half], vectors[..., half:])
    return jnp.concatenate(
        [first * cosine - second * sine, second * cosine + first * sine], axis=-1
    )


def keys_in_place(plain_keys, angle):
    wide_keys = plain_keys.astype(jnp.float32)
    return apply_rotary(wide_keys, angle)


def per_device(raw_keys, raw_values, turn_angle):
    my_angles = lax.dynamic_slice_in_dim(
        turn_angle, lax.axis_index(("farcp", "nearcp")) * raw_keys.shape[1], raw_keys.shape[1]
    )
    sent_keys = keys_in_place(raw_keys, my_angles).astype(jnp.bfloat16)
    moved_keys, stored_values = in_one_piece((sent_keys, raw_values), ("farcp", "nearcp"), 0, 1, 2)
    page_view = moved_keys.reshape(
        moved_keys.shape[0], -1, PAGE, moved_keys.shape[2], moved_keys.shape[3]
    )
    page_high = jnp.max(page_view, axis=2)
    page_low = jnp.min(page_view, axis=2)
    stored_keys = jnp.transpose(moved_keys, (0, 2, 3, 1))
    return (stored_keys, stored_values, page_high, page_low)


def solution(mesh):
    return jax.shard_map(
        per_device,
        mesh=mesh,
        in_specs=(
            P(None, ("farcp", "nearcp"), "heads", None),
            P(None, ("farcp", "nearcp"), "heads", None),
            P(),
        ),
        out_specs=(
            P(("farcp", "nearcp"), "heads", None, None),
            P(("farcp", "nearcp"), None, "heads", None),
            P(("farcp", "nearcp"), None, "heads", None),
            P(("farcp", "nearcp"), None, "heads", None),
        ),
        check_vma=False,
    )
```

profile of v0, /device:TPU:10, one launch (start us, length us, event | category | flops | bytes accessed | tf_op | source)
XLA Modules:
  0.0 187.3 jit_solution(8566229527832821932)
XLA Ops:
  0.6 2.3 %dynamic-slice_cosine_fusion = (f32[1536,64]{0,1:T(8,128)S(1)}, f32[1536,64]{0,1:T(8,128)S(1)}) fusion(f32[24576,64]{0,1:T(8,128)} %param.5, s32[]{:T(128)S(6)} %select_n.3), kind=kLoop, calls=%fused_computation.4 | loop fusion | bytes 1179652 | tf_op jit(solution)/shard_map/cos | solution.py:24
  3.0 1.2 copy.7
  4.1 1.2 copy.8
  5.3 4.0 %convert_element_type.12 = f32[16,1536,1,128]{3,1,2,0:T(8,128)S(1)} convert(bf16[16,1536,1,128]{3,1,2,0:T(8,128)(2,1)} %param.3) | non-fusion elementwise | flops 3145728 | bytes 18874368 | tf_op jit(solution)/shard_map/convert_element_type | solution.py:32
  9.3 5.5 %subtract_convert_fusion = (bf16[16,1536,1,64]{3,1,2,0:T(8,128)(2,1)S(1)}, bf16[16,1536,1,64]{3,1,2,0:T(8,128)(2,1)S(1)}) fusion(f32[16,1536,1,128]{3,1,2,0:T(8,128)S(1)} %convert_element_type.12, f32[1536,64]{1,0:T(8,128)} %copy.8, f32[1536,64]{1,0:T(8,128)} %copy.7), kind=kLoop, calls=%fused_computation.2 | loop fusion | flops 12582912 | bytes 19660800 | tf_op jit(solution)/shard_map/convert
  14.9 6.4 %pad_maximum_fusion = bf16[16,1536,2,128]{3,1,2,0:T(8,128)(2,1)S(1)} fusion(bf16[16,1536,1,128]{3,1,2,0:T(8,128)(2,1)} %param.4, bf16[16,1536,1,64]{3,1,2,0:T(8,128)(2,1)S(1)} %get-tuple-element.11, bf16[16,1536,1,64]{3,1,2,0:T(8,128)(2,1)S(1)} %get-tuple-element.10), kind=kLoop, calls=%fused_computation | loop fusion | flops 37748736 | bytes 25165824 | tf_op jit(solution)/shard_map/concatenate | solution.py:10
  21.3 145.5 %all_to_all.12 = bf16[16,1536,2,128]{3,1,2,0:T(8,128)(2,1)S(1)} all-to-all(bf16[16,1536,2,128]{3,1,2,0:T(8,128)(2,1)S(1)} %pad_maximum_fusion), channel_id=1, replica_groups=mesh['farcp'=4,'nearcp'=4,'heads'=8] {'farcp','nearcp'}, dimensions={0} | all-to-all | bytes 25165824 | tf_op jit(solution)/shard_map/all_to_all | solution.py:12
  166.8 1.9 %copy.9 = bf16[16,1536,2,128]{3,1,0,2:T(8,128)(2,1)S(1)} copy(bf16[16,1536,2,128]{3,1,2,0:T(8,128)(2,1)S(1)} %all_to_all.12) | data formatting | bytes 25165824 | tf_op jit(solution)/shard_map/all_to_all | solution.py:12
  168.7 5.3 %fusion.1 = (bf16[1,24576,1,128]{3,1,2,0:T(8,128)(2,1)S(1)}, bf16[1,1,128,24576]{2,3,1,0:T(8,128)(2,1)}, bf16[1,24576,1,128]{3,1,2,0:T(8,128)(2,1)}) fusion(bf16[1,24576,2,128]{3,1,2,0:T(8,128)(2,1)S(1)} %bitcast.6), kind=kLoop, calls=%fused_computation.7 | loop fusion | bytes 31457280 | tf_op jit(solution)/shard_map/slice | solution.py:17
  174.1 4.6 %fusion = (bf16[384,128]{1,0:T(8,128)(2,1)}, bf16[384,128]{1,0:T(8,128)(2,1)}) fusion(bf16[1,384,64,1,128]{4,2,1,3,0:T(8,128)(2,1)S(1)} %bitcast.7), kind=kLoop, calls=%fused_computation.6 | loop fusion | flops 6193152 | bytes 6488064 | tf_op jit(solution)/shard_map/reduce_min | solution.py:46
  178.7 8.6 %copy.10 = bf16[1,1,128,24576]{3,2,1,0:T(8,128)(2,1)} copy(bf16[1,1,128,24576]{2,3,1,0:T(8,128)(2,1)} %get-tuple-element.13) | data formatting | bytes 12582912
where the time goes:
time: 189 us; the launch traced here: 187 us
  blocking collectives  145 us (77%)
  other arithmetic  20.6 us (11%)
  local copies, waits for them, and re-layouts  20.5 us (11%)
    all_to_all x1, blocking collectives, in_one_piece(): lax.all_to_all(both, axis, split_axis=split_dim, concat_axis=concat_dim,...  145 us
    unnamed x1, local copies, waits for them, and re-layouts  8.61 us
    concatenate x1, other arithmetic, in_one_piece(): both = jnp.concatenate(arrays, axis=along)  6.43 us
    another operation x1, other arithmetic  5.51 us
    slice x1, local copies, waits for them, and re-layouts, in_one_piece(): lax.slice_in_dim(filled, at, at + a.shape[along], axis=along)  5.33 us
    reduce_min x1, other arithmetic, per_device(): page_low = jnp.min(page_view, axis=2)  4.64 us
    convert_element_type x1, other arithmetic, keys_in_place(): wide_keys = plain_keys.astype(jnp.float32)  4.04 us

commit v1 on v0

v1 whole, which is shorter than its diff:
```python
import functools

import jax
import jax.numpy as jnp
from jax import lax
from jax.experimental import pallas as pl
from jax.experimental.pallas import tpu as pltpu
from jax.sharding import PartitionSpec as P

PAGE = 64
MESH = pl.DeviceIdType.MESH
ORDER = (
    (2, 1, 0), (2, 0, 0), (2, 1, 1), (2, 0, 1),
    (1, 1, 0), (3, 1, 0), (1, 0, 0), (3, 0, 0),
    (1, 1, 1), (3, 1, 1), (1, 0, 1), (3, 0, 1),
    (0, 1, 0), (0, 1, 1), (0, 0, 1),
)
PIECES = 4
EARLY = 2


def position():
    far, near = lax.axis_index("farcp"), lax.axis_index("nearcp")
    return (near % 2) * 2 + far // 2, near // 2, far % 2


def indices(x, z, core):
    return (x % 2) * 2 + core, z * 2 + x // 2


def exchange(
    keys, values, angle, out_keys, out_values, out_high, out_low,
    block, landed, turn, cosine, sine, high, low,
    send_keys, recv_keys, send_values, recv_values, local,
):
    blocks, rows, size = block.shape
    half = size // 2
    step = rows // PIECES
    x, z, core = position()
    far, near = indices(x, z, core)
    me = far * 4 + near

    def partner(offset):
        dx, dz, dc = offset
        return indices((x + dx) % 4, (z + dz) % 2, (core + dc) % 2)

    barrier = pltpu.get_barrier_semaphore()
    for offset in ORDER:
        f, n = partner(offset)
        pl.semaphore_signal(barrier, inc=1, device_id={"farcp": f, "nearcp": n}, device_id_type=MESH)

    first = pl.multiple_of(me * rows, 128)
    get_angle = pltpu.make_async_copy(angle.at[:, pl.ds(first, rows)], turn, local.at[0])
    get_angle.start()
    get_keys = pltpu.make_async_copy(keys, block, local.at[1])
    get_keys.start()
    own_values = pltpu.make_async_copy(values.at[me], out_values.at[me], local.at[2])
    own_values.start()
    pl.semaphore_wait(barrier, len(ORDER))

    def copy(source, target, send, recv, which, piece):
        f, n = partner(ORDER[which])
        part = pl.ds(piece * step, step)
        return pltpu.make_async_remote_copy(
            source.at[f * 4 + n, part],
            target.at[me, part],
            send.at[which * PIECES + piece],
            recv.at[which * PIECES + piece],
            device_id={"farcp": f, "nearcp": n},
            device_id_type=MESH,
        )

    value_copies, key_copies = [], []
    for piece in range(EARLY):
        for which in range(len(ORDER)):
            value_copies.append(copy(values, out_values, send_values, recv_values, which, piece))
            value_copies[-1].start()

    get_angle.wait()
    c, s = jnp.cos(turn[...]), jnp.sin(turn[...])
    cosine[...] = jnp.concatenate([c, c], axis=0).T
    sine[...] = jnp.concatenate([-s, s], axis=0).T
    get_keys.wait()

    tile = 128
    tiles = rows // tile

    @pl.loop(0, tiles)
    def _(t):
        at = pl.ds(pl.multiple_of(t * tile, tile), tile)
        co, si = cosine[at], sine[at]

        @pl.loop(0, blocks)
        def _(b):
            k = block[b, at].astype(jnp.float32)
            block[b, at] = (k * co + pltpu.roll(k, half, 1) * si).astype(block.dtype)

    @pl.loop(0, tiles)
    def _(t):
        at = pl.ds(pl.multiple_of(t * tile, tile), tile)
        landed[me, at] = block[me, at]

    for piece in range(PIECES):
        for which in range(len(ORDER)):
            key_copies.append(copy(block, landed, send_keys, recv_keys, which, piece))
            key_copies[-1].start()
    for piece in range(EARLY, PIECES):
        for which in range(len(ORDER)):
            value_copies.append(copy(values, out_values, send_values, recv_values, which, piece))
            value_copies[-1].start()

    for one in key_copies:
        one.wait_recv()

    chunk = 8 * PAGE

    @pl.loop(0, blocks * (rows // chunk))
    def _(i):
        b, t = i // (rows // chunk), i % (rows // chunk)
        k = landed[b, pl.ds(pl.multiple_of(t * chunk, chunk), chunk)]
        for j in range(chunk // tile):
            out_keys[:, pl.ds(pl.multiple_of(i * chunk + j * tile, tile), tile)] = k[j * tile : (j + 1) * tile].T
        pages = k.astype(jnp.float32).reshape(chunk // PAGE, PAGE, size)
        to = pl.ds(pl.multiple_of(i * 8, 8), 8)
        high[to] = jnp.max(pages, axis=1)
        low[to] = jnp.min(pages, axis=1)

    out_high[...] = high[...].astype(out_high.dtype)
    out_low[...] = low[...].astype(out_low.dtype)

    own_values.wait()
    for one in value_copies:
        one.wait_recv()
    for one in key_copies + value_copies:
        one.wait_send()


def per_device(raw_keys, raw_values, turn_angle):
    blocks, rows, _, size = raw_keys.shape
    length = blocks * rows
    kind = raw_keys.dtype
    keys = raw_keys.reshape(blocks, rows, size)
    values = raw_values.reshape(blocks, rows, size)
    angle = turn_angle.T
    anywhere = pl.BlockSpec(memory_space=pl.ANY)
    inside = pl.BlockSpec(memory_space=pltpu.VMEM)
    many = len(ORDER) * PIECES
    moved = pl.pallas_call(
        exchange,
        out_shape=(
            pltpu.VMEM((size, length), kind),
            pltpu.VMEM((blocks, rows, size), kind),
            pltpu.VMEM((length // PAGE, size), kind),
            pltpu.VMEM((length // PAGE, size), kind),
        ),
        in_specs=[anywhere] * 3,
        out_specs=(inside,) * 4,
        scratch_shapes=[
            pltpu.VMEM((blocks, rows, size), kind),
            pltpu.VMEM((blocks, rows, size), kind),
            pltpu.VMEM((size // 2, rows), jnp.float32),
            pltpu.VMEM((rows, size), jnp.float32),
            pltpu.VMEM((rows, size), jnp.float32),
            pltpu.VMEM((length // PAGE, size), jnp.float32),
            pltpu.VMEM((length // PAGE, size), jnp.float32),
        ]
        + [pltpu.SemaphoreType.DMA((many,))] * 4
        + [pltpu.SemaphoreType.DMA((3,))],
        compiler_params=pltpu.CompilerParams(
            collective_id=0, has_side_effects=True, vmem_limit_bytes=48 << 20
        ),
    )(keys, values, angle)
    k, v, high, low = moved
    return k[None, None], v.reshape(1, length, 1, size), high[None, :, None], low[None, :, None]


def solution(mesh):
    return jax.shard_map(
        per_device,
        mesh=mesh,
        in_specs=(
            P(None, ("farcp", "nearcp"), "heads", None),
            P(None, ("farcp", "nearcp"), "heads", None),
            P(),
        ),
        out_specs=(
            P(("farcp", "nearcp"), "heads", None, None),
            P(("farcp", "nearcp"), None, "heads", None),
            P(("farcp", "nearcp"), None, "heads", None),
            P(("farcp", "nearcp"), None, "heads", None),
        ),
        check_vma=False,
    )
```

time: 189 us -> 153 us (0.81)
  Pallas kernels: 0 us -> 145 us
  blocking collectives: 145 us -> 0 us
  other arithmetic: 20.6 us -> 0 us
  local copies, waits for them, and re-layouts: 20.5 us -> 6.69 us
    all_to_all x1 -> x0, blocking collectives: 145 us -> none  [in_one_piece(): lax.all_to_all(both, axis, split_axis=split_dim, concat_axis=concat_dim,...]
    pallas_call x0 -> x1, Pallas kernels: none -> 145 us  [per_device(): pl.pallas_call(exchange, out_shape=(pltpu.VMEM((size, length), kind), plt...]
    concatenate x1 -> x0, other arithmetic: 6.43 us -> none  [in_one_piece(): both = jnp.concatenate(arrays, axis=along)]
    another operation x1 -> x0, other arithmetic: 5.51 us -> none
    slice x1 -> x0, local copies, waits for them, and re-layouts: 5.33 us -> none  [in_one_piece(): lax.slice_in_dim(filled, at, at + a.shape[along], axis=along)]
    reduce_min x1 -> x0, other arithmetic: 4.64 us -> none  [per_device(): page_low = jnp.min(page_view, axis=2)]
    convert_element_type x1 -> x0, other arithmetic: 4.04 us -> none  [keys_in_place(): wide_keys = plain_keys.astype(jnp.float32)]
    cos x2 -> x0, local copies, waits for them, and re-layouts: 3.49 us -> none  [apply_rotary(): jnp.cos(angle)[None, :, None, :]]
where the time goes in v1:
time: 153 us; the launch traced here: 152 us
  Pallas kernels  145 us (95%)
  local copies, waits for them, and re-layouts  6.69 us (4%)
    pallas_call x1, Pallas kernels, per_device(): pl.pallas_call(exchange, out_shape=(pltpu.VMEM((size, length), kind), plt...  145 us
    unnamed x4, local copies, waits for them, and re-layouts  6.69 us

profile of v1, /device:TPU:10, one launch (start us, length us, event | category | flops | bytes accessed | tf_op | source)
XLA Modules:
  0.0 151.9 jit_solution(13250452571024846828)
XLA Ops:
  0.6 144.5 %shard_map.66 = (bf16[128,24576]{1,0:T(8,128)(2,1)S(1)}, bf16[16,1536,128]{2,1,0:T(8,128)(2,1)S(1)}, bf16[384,128]{1,0:T(8,128)(2,1)S(1)}, bf16[384,128]{1,0:T(8,128)(2,1)S(1)}) custom-call(bf16[16,1536,128]{2,1,0:T(8,128)(2,1)} %bitcast.11, bf16[16,1536,128]{2,1,0:T(8,128)(2,1)} %bitcast.12, f32[64,24576]{1,0:T(8,128)} %bitcast.13), custom_call_target="tpu_custom_call" | custom-call | tf_op jit(solution)/shard_map/pallas_call | solution.py:148
  145.2 2.7 %copy.11 = bf16[1,1,128,24576]{3,2,1,0:T(8,128)(2,1)} copy(bf16[1,1,128,24576]{3,2,1,0:T(8,128)(2,1)S(1)} %bitcast.8) | data formatting | bytes 12582912
  147.9 2.7 %copy.12 = bf16[1,24576,1,128]{3,1,2,0:T(8,128)(2,1)} copy(bf16[1,24576,1,128]{3,1,2,0:T(8,128)(2,1)S(1)} %bitcast.7) | data formatting | bytes 12582912
  150.6 0.6 copy.13
  151.2 0.6 copy.14

commit v2 on v1

--- a/solution.py
+++ b/solution.py
@@ -10,10 +10,10 @@
 PAGE = 64
 MESH = pl.DeviceIdType.MESH
 ORDER = (
-    (2, 1, 0), (2, 0, 0), (2, 1, 1), (2, 0, 1),
-    (1, 1, 0), (3, 1, 0), (1, 0, 0), (3, 0, 0),
-    (1, 1, 1), (3, 1, 1), (1, 0, 1), (3, 0, 1),
-    (0, 1, 0), (0, 1, 1), (0, 0, 1),
+    (2, 1, 0, 0), (2, 0, 0, 0), (2, 1, 1, 0), (2, 0, 1, 0),
+    (1, 1, 0, 0), (3, 1, 0, 0), (1, 0, 0, 0), (3, 0, 0, 0),
+    (1, 1, 1, 0), (3, 1, 1, 0), (1, 0, 1, 0), (3, 0, 1, 0),
+    (0, 1, 0, 0), (0, 1, 1, 0), (0, 0, 1, 0),
 )
 PIECES = 4
 EARLY = 2
@@ -30,7 +30,7 @@
 
 def exchange(
     keys, values, angle, out_keys, out_values, out_high, out_low,
-    block, landed, turn, cosine, sine, high, low,
+    staged, block, landed, turn, cosine, sine, high, low,
     send_keys, recv_keys, send_values, recv_values, local,
 ):
     blocks, rows, size = block.shape
@@ -41,9 +41,11 @@
     me = far * 4 + near
 
     def partner(offset):
-        dx, dz, dc = offset
-        return indices((x + dx) % 4, (z + dz) % 2, (core + dc) % 2)
-
+        dx, dz, dc, turned = offset
+        return indices((x + dx) % 4, (z + dz + turned * core) % 2, (core + dc) % 2)
+
+    get_values = pltpu.make_async_copy(values.at[:, pl.ds(0, EARLY * step)], staged, local.at[3])
+    get_values.start()
     barrier = pltpu.get_barrier_semaphore()
     for offset in ORDER:
         f, n = partner(offset)
@@ -57,6 +59,7 @@
     own_values = pltpu.make_async_copy(values.at[me], out_values.at[me], local.at[2])
     own_values.start()
     pl.semaphore_wait(barrier, len(ORDER))
+    get_values.wait()
 
     def copy(source, target, send, recv, which, piece):
         f, n = partner(ORDER[which])
@@ -64,17 +67,15 @@
         return pltpu.make_async_remote_copy(
             source.at[f * 4 + n, part],
             target.at[me, part],
-            send.at[which * PIECES + piece],
-            recv.at[which * PIECES + piece],
+            send,
+            recv,
             device_id={"farcp": f, "nearcp": n},
             device_id_type=MESH,
         )
 
-    value_copies, key_copies = [], []
     for piece in range(EARLY):
         for which in range(len(ORDER)):
-            value_copies.append(copy(values, out_values, send_values, recv_values, which, piece))
-            value_copies[-1].start()
+            copy(staged, out_values, send_values, recv_values, which, piece).start()
 
     get_angle.wait()
     c, s = jnp.cos(turn[...]), jnp.sin(turn[...])
@@ -102,15 +103,25 @@
 
     for piece in range(PIECES):
         for which in range(len(ORDER)):
-            key_copies.append(copy(block, landed, send_keys, recv_keys, which, piece))
-            key_copies[-1].start()
+            copy(block, landed, send_keys, recv_keys, which, piece).start()
     for piece in range(EARLY, PIECES):
         for which in range(len(ORDER)):
-            value_copies.append(copy(values, out_values, send_values, recv_values, which, piece))
-            value_copies[-1].start()
-
-    for one in key_copies:
-        one.wait_recv()
+            copy(values, out_values, send_values, recv_values, which, piece).start()
+
+    def all_of(source, target, send, recv):
+        every = pl.ds(0, len(ORDER))
+        return pltpu.make_async_remote_copy(
+            source.at[every],
+            target.at[every],
+            send,
+            recv,
+            device_id={"farcp": far, "nearcp": near},
+            device_id_type=MESH,
+        )
+
+    all_keys = all_of(block, landed, send_keys, recv_keys)
+    all_values = all_of(values, out_values, send_values, recv_values)
+    all_keys.wait_recv()
 
     chunk = 8 * PAGE
 
@@ -129,10 +140,21 @@
     out_low[...] = low[...].astype(out_low.dtype)
 
     own_values.wait()
-    for one in value_copies:
-        one.wait_recv()
-    for one in key_copies + value_copies:
-        one.wait_send()
+    all_keys.wait_send()
+    all_values.wait_send()
+    all_values.wait_recv()
+
+
+def write_out(keys, values, high, low, out_keys, out_values, out_high, out_low, done):
+    copies = [(high, out_high), (low, out_low)]
+    for a, b in ((keys, out_keys), (values, out_values)):
+        step = a.shape[0] // 8
+        copies += [(a.at[pl.ds(i * step, step)], b.at[pl.ds(i * step, step)]) for i in range(8)]
+    copies = [pltpu.make_async_copy(a, b, done.at[i]) for i, (a, b) in enumerate(copies)]
+    for one in copies:
+        one.start()
+    for one in copies:
+        one.wait()
 
 
 def per_device(raw_keys, raw_values, turn_angle):
@@ -144,7 +166,6 @@
     angle = turn_angle.T
     anywhere = pl.BlockSpec(memory_space=pl.ANY)
     inside = pl.BlockSpec(memory_space=pltpu.VMEM)
-    many = len(ORDER) * PIECES
     moved = pl.pallas_call(
         exchange,
         out_shape=(
@@ -156,6 +177,7 @@
         in_specs=[anywhere] * 3,
         out_specs=(inside,) * 4,
         scratch_shapes=[
+            pltpu.VMEM((blocks, rows // PIECES * EARLY, size), kind),
             pltpu.VMEM((blocks, rows, size), kind),
             pltpu.VMEM((blocks, rows, size), kind),
             pltpu.VMEM((size // 2, rows), jnp.float32),
@@ -164,14 +186,23 @@
             pltpu.VMEM((length // PAGE, size), jnp.float32),
             pltpu.VMEM((length // PAGE, size), jnp.float32),
         ]
-        + [pltpu.SemaphoreType.DMA((many,))] * 4
-        + [pltpu.SemaphoreType.DMA((3,))],
+        + [pltpu.SemaphoreType.DMA] * 4
+        + [pltpu.SemaphoreType.DMA((4,))],
         compiler_params=pltpu.CompilerParams(
             collective_id=0, has_side_effects=True, vmem_limit_bytes=48 << 20
         ),
     )(keys, values, angle)
     k, v, high, low = moved
-    return k[None, None], v.reshape(1, length, 1, size), high[None, :, None], low[None, :, None]
+    moved = [pltpu.with_memory_space_constraint(a, pltpu.VMEM) for a in (k, v.reshape(length, size), high, low)]
+    k, v, high, low = pl.pallas_call(
+        write_out,
+        out_shape=tuple(pltpu.HBM(a.shape, a.dtype) for a in moved),
+        in_specs=[inside] * 4,
+        out_specs=(anywhere,) * 4,
+        scratch_shapes=[pltpu.SemaphoreType.DMA((18,))],
+        compiler_params=pltpu.CompilerParams(vmem_limit_bytes=1 << 20),
+    )(*moved)
+    return k[None, None], v[None, :, None], high[None, :, None], low[None, :, None]
 
 
 def solution(mesh):

time: 153 us -> 148 us (0.967)
  local copies, waits for them, and re-layouts: 6.69 us -> 0 us
  Pallas kernels: 145 us -> 147 us
    unnamed x4 -> x0, local copies, waits for them, and re-layouts: 6.69 us -> none
    pallas_call x0 -> x1, Pallas kernels: none -> 4.78 us  [per_device(): pl.pallas_call(write_out, out_shape=tuple((pltpu.HBM(a.shape, a.dtype) fo...]
    pallas_call x1, Pallas kernels: 145 us -> 142 us  [per_device(): pl.pallas_call(exchange, out_shape=(pltpu.VMEM((size, length), kind), plt...]
where the time goes in v2:
time: 148 us; the launch traced here: 147 us
  Pallas kernels  147 us (99%)
    pallas_call x1, Pallas kernels, per_device(): pl.pallas_call(exchange, out_shape=(pltpu.VMEM((size, length), kind), plt...  142 us
    pallas_call x1, Pallas kernels, per_device(): pl.pallas_call(write_out, out_shape=tuple((pltpu.HBM(a.shape, a.dtype) fo...  4.78 us

profile of v2, /device:TPU:10, one launch (start us, length us, event | category | flops | bytes accessed | tf_op | source)
XLA Modules:
  0.0 147.5 jit_solution(12715437430910807147)
XLA Ops:
  0.6 142.0 %shard_map.66 = (bf16[128,24576]{1,0:T(8,128)(2,1)S(1)}, bf16[16,1536,128]{2,1,0:T(8,128)(2,1)S(1)}, bf16[384,128]{1,0:T(8,128)(2,1)S(1)}, bf16[384,128]{1,0:T(8,128)(2,1)S(1)}) custom-call(bf16[16,1536,128]{2,1,0:T(8,128)(2,1)} %bitcast.9, bf16[16,1536,128]{2,1,0:T(8,128)(2,1)} %bitcast.10, f32[64,24576]{1,0:T(8,128)} %bitcast.11), custom_call_target="tpu_custom_call" | custom-call | tf_op jit(solution)/shard_map/pallas_call | solution.py:169
  142.7 4.8 %shard_map.67 = (bf16[128,24576]{1,0:T(8,128)(2,1)}, bf16[24576,128]{1,0:T(8,128)(2,1)}, bf16[384,128]{1,0:T(8,128)(2,1)}, bf16[384,128]{1,0:T(8,128)(2,1)}) custom-call(bf16[128,24576]{1,0:T(8,128)(2,1)S(1)} %get-tuple-element.12.keys, bf16[24576,128]{1,0:T(8,128)(2,1)S(1)} %bitcast.8, bf16[384,128]{1,0:T(8,128)(2,1)S(1)} %get-tuple-element.14.high, ...), custom_call_target="tpu_custom_call" | custom-call | tf_op jit(solution)/shard_map/pallas_call | solution.py:197

commit v3 on v2

--- a/solution.py
+++ b/solution.py
@@ -15,8 +15,8 @@
     (1, 1, 1, 0), (3, 1, 1, 0), (1, 0, 1, 0), (3, 0, 1, 0),
     (0, 1, 0, 0), (0, 1, 1, 0), (0, 0, 1, 0),
 )
-PIECES = 4
-EARLY = 2
+PIECES = 8
+EARLY = 3
 
 
 def position():
@@ -31,7 +31,7 @@
 def exchange(
     keys, values, angle, out_keys, out_values, out_high, out_low,
     staged, block, landed, turn, cosine, sine, high, low,
-    send_keys, recv_keys, send_values, recv_values, local,
+    for_early, for_keys, for_across, for_along, local,
 ):
     blocks, rows, size = block.shape
     half = size // 2
@@ -61,21 +61,21 @@
     pl.semaphore_wait(barrier, len(ORDER))
     get_values.wait()
 
-    def copy(source, target, send, recv, which, piece):
-        f, n = partner(ORDER[which])
+    def copy(source, target, semaphores, offset, piece):
+        f, n = partner(offset)
         part = pl.ds(piece * step, step)
         return pltpu.make_async_remote_copy(
             source.at[f * 4 + n, part],
             target.at[me, part],
-            send,
-            recv,
+            semaphores.at[0],
+            semaphores.at[1],
             device_id={"farcp": f, "nearcp": n},
             device_id_type=MESH,
         )
 
     for piece in range(EARLY):
-        for which in range(len(ORDER)):
-            copy(staged, out_values, send_values, recv_values, which, piece).start()
+        for offset in ORDER:
+            copy(staged, out_values, for_early, offset, piece).start()
 
     get_angle.wait()
     c, s = jnp.cos(turn[...]), jnp.sin(turn[...])
@@ -102,27 +102,33 @@
         landed[me, at] = block[me, at]
 
     for piece in range(PIECES):
-        for which in range(len(ORDER)):
-            copy(block, landed, send_keys, recv_keys, which, piece).start()
+        for offset in ORDER:
+            copy(block, landed, for_keys, offset, piece).start()
+    across = [offset for offset in ORDER if offset[2]]
+    along = [offset for offset in ORDER if not offset[2]]
     for piece in range(EARLY, PIECES):
-        for which in range(len(ORDER)):
-            copy(values, out_values, send_values, recv_values, which, piece).start()
-
-    def all_of(source, target, send, recv):
-        every = pl.ds(0, len(ORDER))
+        for offset in across:
+            copy(values, out_values, for_across, offset, piece).start()
+
+    @pl.when(core == 1)
+    def _():
+        for piece in range(EARLY, PIECES):
+            for offset in along:
+                copy(values, out_values, for_along, offset, piece).start()
+
+    def all_of(source, target, semaphores, partners, pieces):
+        every = (pl.ds(0, len(partners)), pl.ds(0, pieces * step))
         return pltpu.make_async_remote_copy(
             source.at[every],
             target.at[every],
-            send,
-            recv,
+            semaphores.at[0],
+            semaphores.at[1],
             device_id={"farcp": far, "nearcp": near},
             device_id_type=MESH,
         )
 
-    all_keys = all_of(block, landed, send_keys, recv_keys)
-    all_values = all_of(values, out_values, send_values, recv_values)
+    all_keys = all_of(block, landed, for_keys, ORDER, PIECES)
     all_keys.wait_recv()
-
     chunk = 8 * PAGE
 
     @pl.loop(0, blocks * (rows // chunk))
@@ -140,9 +146,77 @@
     out_low[...] = low[...].astype(out_low.dtype)
 
     own_values.wait()
+    all_early = all_of(staged, out_values, for_early, ORDER, EARLY)
+    all_early.wait()
     all_keys.wait_send()
-    all_values.wait_send()
-    all_values.wait_recv()
+    all_across = all_of(values, out_values, for_across, across, PIECES - EARLY)
+    all_across.wait()
+
+    @pl.when(core == 1)
+    def _():
+        all_along = all_of(values, out_values, for_along, along, PIECES - EARLY)
+        all_along.wait()
+
+
+def exchange_late(values, after, late, semaphores):
+    del after
+    blocks, rows, _ = late.shape
+    x, z, core = position()
+    far, near = indices(x, z, core)
+    along = [offset for offset in ORDER if not offset[2]]
+
+    def partner(offset):
+        f, n = indices((x + offset[0]) % 4, (z + offset[1]) % 2, core)
+        return f * 4 + n, {"farcp": f, "nearcp": n}
+
+    @pl.when(core == 0)
+    def _():
+        barrier = pltpu.get_barrier_semaphore()
+        for offset in along:
+            _, device = partner(offset)
+            pl.semaphore_signal(barrier, inc=1, device_id=device, device_id_type=MESH)
+        pl.semaphore_wait(barrier, len(along))
+        step = rows // (PIECES - EARLY)
+        for piece in range(PIECES - EARLY):
+            for offset in along:
+                to, device = partner(offset)
+                pltpu.make_async_remote_copy(
+                    values.at[to, pl.ds(values.shape[1] - rows + piece * step, step)],
+                    late.at[far * 4 + near, pl.ds(piece * step, step)],
+                    semaphores.at[0],
+                    semaphores.at[1],
+                    device_id=device,
+                    device_id_type=MESH,
+                ).start()
+        every = (pl.ds(0, len(along)), pl.ds(0, rows))
+        pltpu.make_async_remote_copy(
+            values.at[every],
+            late.at[every],
+            semaphores.at[0],
+            semaphores.at[1],
+            device_id={"farcp": far, "nearcp": near},
+            device_id_type=MESH,
+        ).wait()
+
+
+def write_late(late, _, values, done):
+    rows = late.shape[1]
+    x, z, core = position()
+
+    @pl.when(core == 0)
+    def _():
+        copies = []
+        for i, offset in enumerate([offset for offset in ORDER if not offset[2]]):
+            f, n = indices((x + offset[0]) % 4, (z + offset[1]) % 2, core)
+            b = f * 4 + n
+            copies.append(
+                pltpu.make_async_copy(
+                    late.at[b], values.at[b, pl.ds(values.shape[1] - rows, rows)], done.at[i]
+                )
+            )
+            copies[-1].start()
+        for one in copies:
+            one.wait()
 
 
 def write_out(keys, values, high, low, out_keys, out_values, out_high, out_low, done):
@@ -186,14 +260,14 @@
             pltpu.VMEM((length // PAGE, size), jnp.float32),
             pltpu.VMEM((length // PAGE, size), jnp.float32),
         ]
-        + [pltpu.SemaphoreType.DMA] * 4
+        + [pltpu.SemaphoreType.DMA((2,))] * 4
         + [pltpu.SemaphoreType.DMA((4,))],
         compiler_params=pltpu.CompilerParams(
             collective_id=0, has_side_effects=True, vmem_limit_bytes=48 << 20
         ),
     )(keys, values, angle)
     k, v, high, low = moved
-    moved = [pltpu.with_memory_space_constraint(a, pltpu.VMEM) for a in (k, v.reshape(length, size), high, low)]
+    moved = [pltpu.with_memory_space_constraint(a, pltpu.VMEM) for a in (k, v, high, low)]
     k, v, high, low = pl.pallas_call(
         write_out,
         out_shape=tuple(pltpu.HBM(a.shape, a.dtype) for a in moved),
@@ -202,7 +276,28 @@
         scratch_shapes=[pltpu.SemaphoreType.DMA((18,))],
         compiler_params=pltpu.CompilerParams(vmem_limit_bytes=1 << 20),
     )(*moved)
-    return k[None, None], v[None, :, None], high[None, :, None], low[None, :, None]
+    last = rows // PIECES * (PIECES - EARLY)
+    late = pl.pallas_call(
+        exchange_late,
+        out_shape=pltpu.VMEM((blocks, last, size), kind),
+        in_specs=[anywhere] * 2,
+        out_specs=inside,
+        scratch_shapes=[pltpu.SemaphoreType.DMA((2,))],
+        compiler_params=pltpu.CompilerParams(
+            collective_id=1, has_side_effects=True, vmem_limit_bytes=58 << 20
+        ),
+    )(values, low)
+    late = pltpu.with_memory_space_constraint(late, pltpu.VMEM)
+    v = pl.pallas_call(
+        write_late,
+        out_shape=pltpu.HBM(v.shape, kind),
+        in_specs=[inside, anywhere],
+        out_specs=anywhere,
+        input_output_aliases={1: 0},
+        scratch_shapes=[pltpu.SemaphoreType.DMA((len(ORDER),))],
+        compiler_params=pltpu.CompilerParams(vmem_limit_bytes=1 << 20),
+    )(late, v)
+    return k[None, None], v.reshape(1, length, 1, size), high[None, :, None], low[None, :, None]
 
 
 def solution(mesh):

time: 148 us -> 144 us (0.973)
  Pallas kernels: 147 us -> 143 us
    pallas_call x1, Pallas kernels: 142 us -> 120 us  [per_device(): pl.pallas_call(exchange, out_shape=(pltpu.VMEM((size, length), kind), plt...]
    pallas_call x0 -> x2, Pallas kernels: none -> 18.3 us  [the longest x1 17 us: per_device(): pl.pallas_call(exchange_late, out_shape=pltpu.VMEM((blocks, last, size),...]
where the time goes in v3:
time: 144 us
  Pallas kernels  143 us (99%)
    pallas_call x1, Pallas kernels, per_device(): pl.pallas_call(exchange, out_shape=(pltpu.VMEM((size, length), kind), plt...  120 us
    pallas_call x1, Pallas kernels, per_device(): pl.pallas_call(exchange_late, out_shape=pltpu.VMEM((blocks, last, size),...  17 us
    pallas_call x1, Pallas kernels, per_device(): pl.pallas_call(write_out, out_shape=tuple((pltpu.HBM(a.shape, a.dtype) fo...  4.78 us

profile of v3, /device:TPU:10, one launch (start us, length us, event | category | flops | bytes accessed | tf_op | source)
XLA Modules:
  0.0 143.8 jit_solution(1827314705616155721)
XLA Ops:
  0.6 120.0 %shard_map.66 = (bf16[128,24576]{1,0:T(8,128)(2,1)S(1)}, bf16[16,1536,128]{2,1,0:T(8,128)(2,1)S(1)}, bf16[384,128]{1,0:T(8,128)(2,1)S(1)}, bf16[384,128]{1,0:T(8,128)(2,1)S(1)}) custom-call(bf16[16,1536,128]{2,1,0:T(8,128)(2,1)} %bitcast.9, bf16[16,1536,128]{2,1,0:T(8,128)(2,1)} %bitcast.7, f32[64,24576]{1,0:T(8,128)} %bitcast.10), custom_call_target="tpu_custom_call" | custom-call | tf_op jit(solution)/shard_map/pallas_call | solution.py:243
  120.7 4.8 %shard_map.67 = (bf16[128,24576]{1,0:T(8,128)(2,1)}, bf16[16,1536,128]{2,1,0:T(8,128)(2,1)}, bf16[384,128]{1,0:T(8,128)(2,1)}, bf16[384,128]{1,0:T(8,128)(2,1)}) custom-call(bf16[128,24576]{1,0:T(8,128)(2,1)S(1)} %get-tuple-element.12.keys, bf16[16,1536,128]{2,1,0:T(8,128)(2,1)S(1)} %get-tuple-element.13.values, ...), custom_call_target="tpu_custom_call" | custom-call | tf_op jit(solution)/shard_map/pallas_call | solution.py:271
  125.5 17.0 %shard_map.68.late = bf16[16,960,128]{2,1,0:T(8,128)(2,1)S(1)} custom-call(bf16[16,1536,128]{2,1,0:T(8,128)(2,1)} %bitcast.8, bf16[384,128]{1,0:T(8,128)(2,1)} %get-tuple-element.17.after), custom_call_target="tpu_custom_call" | custom-call | tf_op jit(solution)/shard_map/pallas_call | solution.py:280
  142.5 1.4 shard_map.69
